TPU v7x, 32 devices: a 4x2x2 block of a 4x4x8 slice. The times are simulated.
32 devices in a mesh: dp: 4 (over y, z), ep: 8 (over x, core).
Axes of the slice: x: 4, y: 2, z: 2, core: 2. Of those that a mesh axis runs over, the one named last changes fastest.
The devices are a block of a 4x4x8 slice.
Arguments:
- hidden: bfloat16 [4096, 2560], P(('dp', 'ep')), parts along dimension 0
- norm_gain: float32 [2560], replicated
- router_w: bfloat16 [2560, 64], replicated
- topk_idx: int32 [4096, 6], P(('dp', 'ep')), parts along dimension 0
- w_gate: bfloat16 [64, 2560, 1536], P('ep')
- w_up: bfloat16 [64, 2560, 1536], P('ep')
- w_down: bfloat16 [64, 1536, 2560], P('ep')
- shared_gate: bfloat16 [2560, 3072], replicated
- shared_up: bfloat16 [2560, 3072], replicated
- shared_down: bfloat16 [3072, 2560], replicated
Outputs:
- output: bfloat16 [4096, 2560], P(('dp', 'ep')), parts along dimension 0
There are 4 independent parts. A program takes and returns all parts, laid end to end along the dimension named above; an argument that names none is the same for every part.
All inputs are finite; a program needn't handle non-finite values.
Results may differ from a plain program's by a relative error of at most 0.00101.
Values are sent between devices in bfloat16 or wider.
A program may use at most 768 MiB of HBM per device.

v0:
```python
import functools

import jax
import jax.numpy as jnp
from jax import lax
from jax.experimental import pallas as pl
from jax.experimental.pallas import tpu as pltpu
from jax.sharding import PartitionSpec as P

NORM_EPS = 1e-6
MESH = pl.DeviceIdType.MESH
F32 = jnp.float32
BF16 = jnp.bfloat16
MAIN = 16
GU_SLOTS = 4
D_SLOTS = 4
FF_CHUNKS = 3
H_CHUNKS = 2


def dot(a, b):
    return jnp.dot(a, b, preferred_element_type=F32)


def iota(shape, axis):
    return lax.broadcasted_iota(jnp.int32, shape, axis)


def moe_kernel(
    group, x_hbm, gain_ref, rw_ref, topk_ref, wg, wu, wd, sg, su, sd, out_hbm,
    gx, xo, back, tail, gu_buf, d_buf, act, normed, acc, w_stack, code_all, sel_tail, out_v,
    x_sem, gu_sem, d_sem, xs_sem, xr_sem, cs_sem, cr_sem, os_sem, or_sem,
):
    tok, hid = x_hbm.shape
    ff = wg.shape[2]
    local = wg.shape[0]
    experts = rw_ref.shape[1]
    rounds = local + 1
    fc, hc = ff // FF_CHUNKS, hid // H_CHUNKS
    shared_units = sg.shape[1] // ff
    half = tok // 2
    chips = group // 2

    me = lax.axis_index("ep")
    chip, core = me // 2, me % 2

    def dev(chip_off, flip):
        return ((chip + chip_off) % chips) * 2 + (core + flip) % 2

    def gu_copies(unit, f, slot, shared):
        if shared:
            cols = pl.ds(pl.multiple_of(unit * ff + f * fc, 128), fc)
            srcs = (sg.at[:, cols], su.at[:, cols])
        else:
            cols = pl.ds(f * fc, fc)
            srcs = (wg.at[unit, :, cols], wu.at[unit, :, cols])
        return [pltpu.make_async_copy(srcs[m], gu_buf.at[slot, m], gu_sem.at[slot, m]) for m in range(2)]

    def d_copy(unit, h, slot, shared):
        cols = pl.ds(h * hc, hc)
        src = sd.at[pl.ds(pl.multiple_of(unit * ff, 16), ff), cols] if shared else wd.at[unit, :, cols]
        return pltpu.make_async_copy(src, d_buf.at[slot], d_sem.at[slot])

    def start_gu(unit, f, slot, shared):
        for copy in gu_copies(unit, f, slot, shared):
            copy.start()

    x_copy = pltpu.make_async_copy(x_hbm, gx.at[me], x_sem)
    x_copy.start()
    for q in range(GU_SLOTS):
        start_gu(q // FF_CHUNKS, q % FF_CHUNKS, q, True)
        if q < D_SLOTS:
            d_copy(q // H_CHUNKS, q % H_CHUNKS, q, True).start()

    barrier = pltpu.get_barrier_semaphore()
    for r in range(1, group):
        pl.semaphore_signal(barrier, inc=1, device_id={"ep": (me + r) % group}, device_id_type=MESH)
    pl.semaphore_wait(barrier, group - 1)

    def x_send(src, part, dst, slot):
        rows = gx.at[src, pl.ds(part * half, half)]
        return pltpu.make_async_remote_copy(
            src_ref=rows, dst_ref=rows, send_sem=xs_sem.at[slot], recv_sem=xr_sem.at[src, part],
            device_id={"ep": dst}, device_id_type=MESH)

    def x_wait(src, part):
        x_send(src, part, me, 0).wait_recv()

    left, right, far, partner = dev(chips - 1, 0), dev(1, 0), dev(2, 0), dev(0, 1)
    x_copy.wait()
    x_sends = [
        (me, 0, right), (me, 1, left), (me, 1, right), (me, 0, left), (me, 0, partner), (me, 1, partner),
        (left, 0, right), (left, 0, partner), (right, 1, left), (right, 1, partner),
        (left, 1, partner), (right, 0, partner), (far, 0, partner), (far, 1, partner),
    ]

    def start_x(lo, hi):
        for slot in range(lo, hi):
            x_send(*x_sends[slot], slot).start()

    start_x(0, 6)

    topk = topk_ref[...]
    lanes = iota((tok, 128), 1)
    chosen = jnp.zeros((tok, 128), F32)
    for j in range(topk.shape[1]):
        chosen = jnp.where(topk[:, j:j + 1] == lanes, 1.0, chosen)
    before = jnp.where(iota((tok, tok), 1) < iota((tok, tok), 0), 1.0, 0.0).astype(BF16)
    code = jnp.where(chosen > 0.5, dot(before, chosen.astype(BF16)), -1.0)
    code_t = code.T[:experts]
    code_all[me] = code_t.reshape(group, local, tok)

    def code_send(dst, r):
        return pltpu.make_async_remote_copy(
            src_ref=code_all.at[me, dst], dst_ref=code_all.at[me, dst], send_sem=cs_sem.at[r], recv_sem=cr_sem.at[me],
            device_id={"ep": dst}, device_id_type=MESH)

    def code_wait(src):
        pltpu.make_async_remote_copy(
            src_ref=code_all.at[src, me], dst_ref=code_all.at[src, me], send_sem=cs_sem.at[0], recv_sem=cr_sem.at[src],
            device_id={"ep": me}, device_id_type=MESH).wait_recv()

    def norm(rows_f32):
        inv_rms = lax.rsqrt(jnp.mean(rows_f32 * rows_f32, axis=-1, keepdims=True) + NORM_EPS)
        return (rows_f32 * inv_rms * gain_ref[...]).astype(BF16)

    x_own = gx[me].astype(F32)
    normed[...] = norm(x_own)
    acc[...] = x_own
    for r in range(1, group):
        code_send((me + r) % group, r).start()

    def unit_step(rows, load_rows, gu_first, d_first, next_gu, next_d, put_out):
        for f in range(FF_CHUNKS):
            slot = (gu_first + f) % GU_SLOTS
            for copy in gu_copies(0, 0, slot, False):
                copy.wait()
            gate = dot(load_rows(), gu_buf[slot, 0])
            up = dot(load_rows(), gu_buf[slot, 1])
            act[pl.ds(0, rows), pl.ds(f * fc, fc)] = (jax.nn.silu(gate) * up).astype(BF16)
            next_gu(f, slot)
        for h in range(H_CHUNKS):
            slot = (d_first + h) % D_SLOTS
            d_copy(0, 0, slot, False).wait()
            put_out(h, dot(act[pl.ds(0, rows), :], d_buf[slot]))
            next_d(h, slot)

    def shared_step(u, carry):
        def next_gu(f, slot):
            ahead = (f + GU_SLOTS) // FF_CHUNKS
            f_next = (f + GU_SLOTS) % FF_CHUNKS

            @pl.when(u + ahead < shared_units)
            def _():
                start_gu(u + ahead, f_next, slot, True)

            @pl.when(u + ahead >= shared_units)
            def _():
                start_gu(u + ahead - shared_units, f_next, slot, False)

        def next_d(h, slot):
            d_copy(u + D_SLOTS // H_CHUNKS - shared_units, h, slot, False).start()

        def put_out(h, value):
            cols = pl.ds(h * hc, hc)
            acc[:, cols] = acc[:, cols] + value

        unit_step(tok, lambda: normed[...], u * FF_CHUNKS, u * H_CHUNKS, next_gu, next_d, put_out)

        @pl.when(u == 0)
        def _():
            x_wait(left, 0)
            start_x(6, 8)
            x_wait(right, 1)
            start_x(8, 10)

        return carry

    lax.fori_loop(0, shared_units, shared_step, 0)
    x_wait(left, 1)
    start_x(10, 11)
    x_wait(right, 0)
    start_x(11, 12)

    logits = dot(normed[...], rw_ref[...])
    peak = jnp.max(logits, axis=-1, keepdims=True)
    grown = jnp.exp(logits - peak)
    probs = grown / jnp.sum(grown, axis=-1, keepdims=True)
    p_hi = probs.astype(BF16)
    rest = probs - p_hi.astype(F32)
    p_mid = rest.astype(BF16)
    p_low = (rest - p_mid.astype(F32)).astype(BF16)
    spread_in = jnp.concatenate([code[:, :experts].astype(BF16), p_hi, p_mid, p_low], axis=0)

    def slot_weights(i, carry):
        lane = iota((1, group * MAIN), 1)
        owner, place = lane // MAIN, lane % MAIN
        extra = MAIN // local
        last = jnp.full((1, group * MAIN), i, jnp.int32) == local
        expert = owner * local + jnp.where(last, place // extra, i)
        rank = jnp.where(last, MAIN + place % extra, place).astype(F32)
        pick = jnp.where(iota((experts, group * MAIN), 0) == expert, 1.0, 0.0).astype(BF16)
        spread = dot(spread_in, pick)
        hit = spread[:tok] == rank
        for part in range(3):
            value = jnp.where(hit, spread[(part + 1) * tok:(part + 2) * tok], 0.0)
            w_stack[i, pl.ds(part * tok, tok), :] = value.astype(BF16)
        return carry

    lax.fori_loop(0, rounds, slot_weights, 0)

    def gather_owner(src):
        codes = code_all[src, me]
        spread = jnp.broadcast_to(codes[:, None, :], (local, MAIN, tok)).reshape(local * MAIN, tok)
        row = iota((local * MAIN, tok), 0)
        place = row % MAIN
        pick = jnp.where(spread == place.astype(F32), 1.0, 0.0).astype(BF16)
        extra = MAIN // local
        want = jnp.where(place // extra == src, MAIN + place % extra, -2).astype(F32)
        sel_tail[src] = jnp.where(spread == want, 1.0, 0.0).astype(BF16)
        rows = norm(dot(pick, gx[src]))
        xo[:, src] = rows.reshape(local, MAIN, hid)

    code_all_waits = [dev(off, flip) for off in range(chips) for flip in range(2) if (off, flip) != (0, 0)]
    for src in code_all_waits:
        code_wait(src)
    for off in (0, 1, chips - 1):
        for part in range(2):
            x_wait(dev(off, 1), part)

    def gather_near(p, carry):
        q = p // 2
        gather_owner(dev(q * (q + 1) // 2, p % 2))
        return carry

    lax.fori_loop(0, 6, gather_near, 0)
    x_wait(far, 0)
    start_x(12, 13)
    x_wait(far, 1)
    start_x(13, 14)
    for part in range(2):
        x_wait(dev(2, 1), part)

    def gather_far(p, carry):
        gather_owner(dev(2, p))
        return carry

    lax.fori_loop(0, 2, gather_far, 0)
    picks = jnp.concatenate([sel_tail[s] for s in range(group)], axis=1)
    rows = norm(dot(picks, gx[...].reshape(group * tok, hid)))
    xo[:, group] = rows.reshape(local, MAIN, hid)

    order = [(2, 0), (2, 1), (1, 0), (chips - 1, 0), (1, 1), (chips - 1, 1), (0, 1)]

    def back_send(i, src_ref, slot, dst):
        return pltpu.make_async_remote_copy(
            src_ref=src_ref, dst_ref=back.at[i, me], send_sem=os_sem.at[i, slot], recv_sem=or_sem.at[i, me],
            device_id={"ep": dst}, device_id_type=MESH)

    def back_wait(i, src):
        pltpu.make_async_remote_copy(
            src_ref=back.at[i, src], dst_ref=back.at[i, src], send_sem=os_sem.at[0, 0], recv_sem=or_sem.at[i, src],
            device_id={"ep": me}, device_id_type=MESH).wait_recv()

    def combine(i):
        for off, flip in order:
            back_wait(i, dev(off, flip))
        for h in range(H_CHUNKS):
            cols = pl.ds(h * hc, hc)
            parts = dot(w_stack[i], back[i, :, :, cols].reshape(group * MAIN, hc))
            acc[:, cols] = acc[:, cols] + (parts[:tok] + (parts[tok:2 * tok] + parts[2 * tok:]))

    def routed_step(i, carry):
        rows = (group + 1) * MAIN

        def next_gu(f, slot):
            ahead = (f + GU_SLOTS) // FF_CHUNKS
            f_next = (f + GU_SLOTS) % FF_CHUNKS

            @pl.when(i + ahead < local)
            def _():
                start_gu(i + ahead, f_next, slot, False)

        def next_d(h, slot):
            ahead = D_SLOTS // H_CHUNKS

            @pl.when(i + ahead < local)
            def _():
                d_copy(i + ahead, h, slot, False).start()

        def put_out(h, value):
            xo[i, :, :, pl.ds(h * hc, hc)] = value.astype(BF16).reshape(group + 1, MAIN, hc)

        unit_step(
            rows, lambda: xo[i].reshape(rows, hid), (i + shared_units) * FF_CHUNKS, (i + shared_units) * H_CHUNKS,
            next_gu, next_d, put_out)
        for slot, (off, flip) in enumerate(order):
            dst = dev(off, flip)
            back_send(i, xo.at[i, dst], slot, dst).start()
        back[i, me] = xo[i, me]

        @pl.when(i >= 2)
        def _():
            combine(i - 2)

        return carry

    lax.fori_loop(0, local, routed_step, 0)

    left_over = xo[:, group].reshape(local * MAIN, hid)
    row, col = iota((local * MAIN, local * MAIN), 0), iota((local * MAIN, local * MAIN), 1)
    extra = MAIN // local
    source = ((row % MAIN) // extra) * MAIN + (row // MAIN) * extra + row % extra
    reorder = jnp.where(col == source, 1.0, 0.0).astype(BF16)
    tail[...] = dot(reorder, left_over).astype(BF16).reshape(group, MAIN, hid)
    for slot, (off, flip) in enumerate(order):
        dst = dev(off, flip)
        back_send(local, tail.at[dst], slot, dst).start()
    back[local, me] = tail[me]

    def combine_step(i, carry):
        combine(i)
        return carry

    lax.fori_loop(local - 2, rounds, combine_step, 0)
    out_v[...] = acc[...].astype(BF16)
    out_copy = pltpu.make_async_copy(out_v, out_hbm, x_sem)
    out_copy.start()

    for slot in range(len(x_sends)):
        x_send(*x_sends[slot], slot).wait_send()
    for r in range(1, group):
        code_send((me + r) % group, r).wait_send()

    def drain(i, carry):
        for slot, (off, flip) in enumerate(order):
            dst = dev(off, flip)
            back_send(i, tail.at[dst], slot, dst).wait_send()
        return carry

    lax.fori_loop(0, rounds, drain, 0)
    out_copy.wait()


def solution(mesh):
    group = mesh.shape["ep"]

    def local_step(hidden, norm_gain, router_w, topk_idx, w_gate, w_up, w_down, shared_gate, shared_up, shared_down):
        tok, hid = hidden.shape
        top_k = topk_idx.shape[1]
        experts = router_w.shape[1]
        local, _, ff = w_gate.shape
        capacity = 3 * tok * top_k // (2 * experts)
        assert group == 8 and (capacity - MAIN) * local == MAIN and local == group
        rounds = local + 1
        fc, hc = ff // FF_CHUNKS, hid // H_CHUNKS
        any_spec = pl.BlockSpec(memory_space=pl.ANY)
        vmem_spec = pl.BlockSpec(memory_space=pltpu.VMEM)
        dma = pltpu.SemaphoreType.DMA
        return pl.pallas_call(
            functools.partial(moe_kernel, group),
            out_shape=jax.ShapeDtypeStruct((tok, hid), BF16),
            in_specs=[any_spec, vmem_spec, vmem_spec, vmem_spec] + [any_spec] * 6,
            out_specs=any_spec,
            scratch_shapes=[
                pltpu.VMEM((group, tok, hid), BF16),
                pltpu.VMEM((local, group + 1, MAIN, hid), BF16),
                pltpu.VMEM((rounds, group, MAIN, hid), BF16),
                pltpu.VMEM((group, MAIN, hid), BF16),
                pltpu.VMEM((GU_SLOTS, 2, hid, fc), BF16),
                pltpu.VMEM((D_SLOTS, ff, hc), BF16),
                pltpu.VMEM(((group + 1) * MAIN, ff), BF16),
                pltpu.VMEM((tok, hid), BF16),
                pltpu.VMEM((tok, hid), F32),
                pltpu.VMEM((rounds, 3 * tok, group * MAIN), BF16),
                pltpu.VMEM((group, group, local, tok), F32),
                pltpu.VMEM((group, local * MAIN, tok), BF16),
                pltpu.VMEM((tok, hid), BF16),
                dma,
                dma((GU_SLOTS, 2)),
                dma((D_SLOTS,)),
                dma((14,)),
                dma((group, 2)),
                dma((group,)),
                dma((group,)),
                dma((rounds, group - 1)),
                dma((rounds, group)),
            ],
            compiler_params=pltpu.CompilerParams(
                collective_id=0, has_side_effects=True, vmem_limit_bytes=67_000_000),
            name="moe_block",
        )(hidden, norm_gain.reshape(1, hid), router_w, topk_idx, w_gate, w_up, w_down, shared_gate, shared_up, shared_down)

    token_spec = P(("dp", "ep"), None)
    expert_spec = P("ep", None, None)
    return jax.shard_map(
        local_step,
        mesh=mesh,
        in_specs=(token_spec, P(None), P(None, None), token_spec, expert_spec, expert_spec, expert_spec,
                  P(None, None), P(None, None), P(None, None)),
        out_specs=token_spec,
        check_vma=False,
    )
```

profile of v0, /device:TPU:81, one launch (start us, length us, event | category | flops | bytes accessed | tf_op | source)
XLA Modules:
  0.0 119.7 jit_solution(979997248675406681)
XLA Ops:
  0.0 1.3 %reshape.3.gain_ref = f32[1,2560]{1,0:T(1,128)} reshape(f32[2560]{0:T(1024)} %param.11) | data formatting | bytes 20480 | tf_op jit(solution)/shard_map/reshape | solution.py:392
  1.3 1.4 %copy.12.topk_ref = s32[128,6]{1,0:T(8,128)} copy(s32[128,6]{0,1:T(8,128)} %param.13) | data formatting | bytes 6144 | tf_op args[3]
  2.7 2.1 %copy.11.rw_ref = bf16[2560,64]{1,0:T(8,128)(2,1)} copy(bf16[2560,64]{0,1:T(8,128)(2,1)} %param.12) | data formatting | bytes 655360 | tf_op args[2]
  4.8 113.0 %moe_block.1 = bf16[128,2560]{1,0:T(8,128)(2,1)} custom-call(bf16[128,2560]{1,0:T(8,128)(2,1)} %x_hbm.1, f32[1,2560]{1,0:T(1,128)} %reshape.3.gain_ref, bf16[2560,64]{1,0:T(8,128)(2,1)} %copy.11.rw_ref, s32[128,6]{1,0:T(8,128)} %copy.12.topk_ref, bf16[8,2560,1536]{2,1,0:T(8,128)(2,1)} %wg.1, bf16[8,2560,1536]{2,1,0:T(8,128)(2,1)} %wu.1, ...), custom_call_target="tpu_custom_call" | custom-call | tf_op jit(solution)/shard_map/moe_block/pallas_call | solution.py:360
  117.8 2.0 %copy.14 = bf16[128,2560]{1,0:T(8,128)(2,1)} copy(bf16[128,2560]{1,0:T(8,128)(2,1)} %moe_block.1) | data formatting | bytes 1310720
where the time goes:
time: 120 us
  Pallas kernels  113 us (94%)
  local copies, waits for them, and re-layouts  6.74 us (6%)
    pallas_call x1, Pallas kernels, local_step(): pl.pallas_call(functools.partial(moe_kernel, group), out_shape=jax.ShapeD...  113 us
    unnamed x3, local copies, waits for them, and re-layouts  5.43 us

commit v1 on v0

v1 whole, which is shorter than its diff:
```python
import functools

import jax
import jax.numpy as jnp
from jax import lax
from jax.experimental import pallas as pl
from jax.experimental.pallas import tpu as pltpu
from jax.sharding import PartitionSpec as P

NORM_EPS = 1e-6
MESH = pl.DeviceIdType.MESH
F32 = jnp.float32
BF16 = jnp.bfloat16
MAIN = 16
GU_SLOTS = 4
D_SLOTS = 4
FF_CHUNKS = 3
H_CHUNKS = 2


def dot(a, b):
    return jnp.dot(a, b, preferred_element_type=F32)


def iota(shape, axis):
    return lax.broadcasted_iota(jnp.int32, shape, axis)


def moe_kernel(
    group, x_hbm, gain_hbm, rw_hbm, topk_hbm, wg, wu, wd, sg, su, sd, out_hbm,
    gx, xo, back, tail, gu_buf, d_buf, act, normed, acc, w_stack, code_all, sel_tail, tail_sum,
    gain_ref, rw_ref, topk_ref, in_sem, x_sem, gu_sem, d_sem, xs_sem, xr_sem, cs_sem, cr_sem, os_sem, or_sem,
):
    tok, hid = x_hbm.shape
    ff = wg.shape[2]
    local = wg.shape[0]
    experts = rw_hbm.shape[0]
    rounds = local + 1
    fc, hc = ff // FF_CHUNKS, hid // H_CHUNKS
    shared_units = sg.shape[1] // ff
    half = tok // 2
    chips = group // 2

    me = lax.axis_index("ep")
    chip, core = me // 2, me % 2

    def dev(chip_off, flip):
        return ((chip + chip_off) % chips) * 2 + (core + flip) % 2

    def gu_copies(unit, f, slot, shared):
        if shared:
            cols = pl.ds(pl.multiple_of(unit * ff + f * fc, 128), fc)
            srcs = (sg.at[:, cols], su.at[:, cols])
        else:
            cols = pl.ds(f * fc, fc)
            srcs = (wg.at[unit, :, cols], wu.at[unit, :, cols])
        return [pltpu.make_async_copy(srcs[m], gu_buf.at[slot, m], gu_sem.at[slot, m]) for m in range(2)]

    def d_copy(unit, h, slot, shared):
        cols = pl.ds(h * hc, hc)
        src = sd.at[pl.ds(pl.multiple_of(unit * ff, 16), ff), cols] if shared else wd.at[unit, :, cols]
        return pltpu.make_async_copy(src, d_buf.at[slot], d_sem.at[slot])

    def start_gu(unit, f, slot, shared):
        for copy in gu_copies(unit, f, slot, shared):
            copy.start()

    x_copy = pltpu.make_async_copy(x_hbm, gx.at[me], x_sem)
    x_copy.start()
    small = [
        pltpu.make_async_copy(topk_hbm, topk_ref, in_sem.at[0]),
        pltpu.make_async_copy(gain_hbm, gain_ref, in_sem.at[1]),
        pltpu.make_async_copy(rw_hbm, rw_ref, in_sem.at[2]),
    ]
    for copy in small:
        copy.start()

    barrier = pltpu.get_barrier_semaphore()
    for r in range(1, group):
        pl.semaphore_signal(barrier, inc=1, device_id={"ep": (me + r) % group}, device_id_type=MESH)
    x_copy.wait()
    for q in range(GU_SLOTS):
        start_gu(q // FF_CHUNKS, q % FF_CHUNKS, q, True)
        if q < D_SLOTS:
            d_copy(q // H_CHUNKS, q % H_CHUNKS, q, True).start()

    for copy in small:
        copy.wait()
    line = iota((tok, tok), 0)
    chosen = jnp.zeros((tok, tok), F32)
    for j in range(topk_ref.shape[0]):
        chosen = jnp.where(topk_ref[j:j + 1, :] == line, 1.0, chosen)
    before = jnp.where(line < iota((tok, tok), 1), 1.0, 0.0).astype(BF16)
    code_t = jnp.where(chosen > 0.5, dot(chosen.astype(BF16), before), -1.0)
    code_all[me] = code_t[:experts].reshape(group, local, tok)
    code = code_t.T

    gain = gain_ref[...].reshape(1, hid)

    def norm(rows_f32):
        inv_rms = lax.rsqrt(jnp.mean(rows_f32 * rows_f32, axis=-1, keepdims=True) + NORM_EPS)
        return (rows_f32 * inv_rms * gain).astype(BF16)

    x_own = gx[me].astype(F32)
    normed[...] = norm(x_own)
    acc[...] = x_own

    pl.semaphore_wait(barrier, group - 1)

    def code_send(dst, r):
        return pltpu.make_async_remote_copy(
            src_ref=code_all.at[me, dst], dst_ref=code_all.at[me, dst], send_sem=cs_sem.at[r], recv_sem=cr_sem.at[me],
            device_id={"ep": dst}, device_id_type=MESH)

    def code_wait(src):
        pltpu.make_async_remote_copy(
            src_ref=code_all.at[src, me], dst_ref=code_all.at[src, me], send_sem=cs_sem.at[0], recv_sem=cr_sem.at[src],
            device_id={"ep": me}, device_id_type=MESH).wait_recv()

    for r in range(1, group):
        code_send((me + r) % group, r).start()

    def x_send(src, part, dst, slot):
        rows = gx.at[src, pl.ds(part * half, half)]
        return pltpu.make_async_remote_copy(
            src_ref=rows, dst_ref=rows, send_sem=xs_sem.at[slot], recv_sem=xr_sem.at[src, part],
            device_id={"ep": dst}, device_id_type=MESH)

    def x_wait(src, part):
        x_send(src, part, me, 0).wait_recv()

    left, right, far, partner = dev(chips - 1, 0), dev(1, 0), dev(2, 0), dev(0, 1)
    x_sends = [
        (me, 0, right), (me, 1, left), (me, 1, right), (me, 0, left), (me, 0, partner), (me, 1, partner),
        (left, 0, right), (left, 0, partner), (right, 1, left), (right, 1, partner),
        (left, 1, partner), (right, 0, partner), (far, 0, partner), (far, 1, partner),
    ]

    def start_x(lo, hi):
        for slot in range(lo, hi):
            x_send(*x_sends[slot], slot).start()

    start_x(0, 6)

    logits = lax.dot_general(normed[...], rw_ref[...], (((1,), (1,)), ((), ())), preferred_element_type=F32)
    peak = jnp.max(logits, axis=-1, keepdims=True)
    grown = jnp.exp(logits - peak)
    probs = grown / jnp.sum(grown, axis=-1, keepdims=True)
    p_hi = probs.astype(BF16)
    rest = probs - p_hi.astype(F32)
    p_mid = rest.astype(BF16)
    p_low = (rest - p_mid.astype(F32)).astype(BF16)
    spread_in = jnp.concatenate([code[:, :experts].astype(BF16), p_hi, p_mid, p_low], axis=0)

    def slot_weights(i, carry):
        lane = iota((1, group * MAIN), 1)
        owner, place = lane // MAIN, lane % MAIN
        extra = MAIN // local
        last = jnp.full((1, group * MAIN), i, jnp.int32) == local
        expert = owner * local + jnp.where(last, place // extra, i)
        rank = jnp.where(last, MAIN + place % extra, place).astype(F32)
        pick = jnp.where(iota((experts, group * MAIN), 0) == expert, 1.0, 0.0).astype(BF16)
        spread = dot(spread_in, pick)
        hit = spread[:tok] == rank
        for part in range(3):
            value = jnp.where(hit, spread[(part + 1) * tok:(part + 2) * tok], 0.0)
            w_stack[i, pl.ds(part * tok, tok), :] = value.astype(BF16)
        return carry

    lax.fori_loop(0, rounds, slot_weights, 0)

    places = [(0, 0), (0, 1), (1, 0), (1, 1), (chips - 1, 0), (chips - 1, 1), (2, 0), (2, 1)]
    owners = [dev(off, flip) for off, flip in places]
    near = 6
    extra = MAIN // local

    def gather_owner(src, p):
        codes = code_all[src, me]
        spread = jnp.broadcast_to(codes[:, None, :], (local, MAIN, tok)).reshape(local * MAIN, tok)
        place = iota((local * MAIN, tok), 0) % MAIN
        pick = jnp.where(spread == place.astype(F32), 1.0, 0.0).astype(BF16)
        want = jnp.where(place // extra == p, MAIN + place % extra, -2).astype(F32)
        sel_tail[p // 2, :, pl.ds(pl.multiple_of(src % 2 * tok, tok), tok)] = jnp.where(spread == want, 1.0, 0.0).astype(BF16)
        rows = norm(dot(pick, gx[src]))
        xo[:, p] = rows.reshape(local, MAIN, hid)

    def gather_extra(pair):
        first = dev(places[2 * pair][0], 0) // 2 * 2
        return dot(sel_tail[pair], gx[pl.ds(first, 2)].reshape(2 * tok, hid))

    for src in owners[1:]:
        code_wait(src)
    for part in range(2):
        x_wait(partner, part)

    def gather_home(p, carry):
        gather_owner(dev(0, p), p)
        return carry

    lax.fori_loop(0, 2, gather_home, 0)
    x_wait(left, 0)
    start_x(6, 8)
    x_wait(right, 1)
    start_x(8, 10)

    def unit_step(rows, load_rows, gu_first, d_first, put_out, next_gu=None, next_d=None, arrived=False):
        for f in range(FF_CHUNKS):
            slot = (gu_first + f) % GU_SLOTS
            if not arrived:
                for copy in gu_copies(0, 0, slot, False):
                    copy.wait()
            gate = dot(load_rows(), gu_buf[slot, 0])
            up = dot(load_rows(), gu_buf[slot, 1])
            act[pl.ds(0, rows), pl.ds(f * fc, fc)] = (jax.nn.silu(gate) * up).astype(BF16)
            if next_gu is not None:
                next_gu(f, slot)
        for h in range(H_CHUNKS):
            slot = (d_first + h) % D_SLOTS
            if not arrived:
                d_copy(0, 0, slot, False).wait()
            put_out(h, dot(act[pl.ds(0, rows), :], d_buf[slot]))
            if next_d is not None:
                next_d(h, slot)

    def shared_step(u, carry):
        def next_gu(f, slot):
            ahead = (f + GU_SLOTS) // FF_CHUNKS
            f_next = (f + GU_SLOTS) % FF_CHUNKS

            @pl.when(u + ahead < shared_units)
            def _():
                start_gu(u + ahead, f_next, slot, True)

            @pl.when(u + ahead >= shared_units)
            def _():
                start_gu(u + ahead - shared_units, f_next, slot, False)

        def next_d(h, slot):
            d_copy(u + D_SLOTS // H_CHUNKS - shared_units, h, slot, False).start()

        def put_out(h, value):
            cols = pl.ds(h * hc, hc)
            acc[:, cols] = acc[:, cols] + value

        unit_step(tok, lambda: normed[...], u * FF_CHUNKS, u * H_CHUNKS, put_out, next_gu, next_d)

        return carry

    lax.fori_loop(0, shared_units, shared_step, 0)
    x_wait(left, 1)
    start_x(10, 11)
    x_wait(right, 0)
    start_x(11, 12)

    def gather_side(core_flip):
        def step(q, carry):
            gather_owner(dev(1 + q * (chips - 2), core_flip), 2 + 2 * q + core_flip)
            return carry

        lax.fori_loop(0, 2, step, 0)

    gather_side(0)
    for off in (1, chips - 1):
        for part in range(2):
            x_wait(dev(off, 1), part)
    gather_side(1)

    send_order = [6, 7, 2, 4, 3, 5, 1]

    def back_send(i, src_ref, p):
        return pltpu.make_async_remote_copy(
            src_ref=src_ref, dst_ref=back.at[i, me], send_sem=os_sem.at[i, p - 1], recv_sem=or_sem.at[i, me],
            device_id={"ep": owners[p]}, device_id_type=MESH)

    def back_wait(i, src):
        pltpu.make_async_remote_copy(
            src_ref=back.at[i, src], dst_ref=back.at[i, src], send_sem=os_sem.at[0, 0], recv_sem=or_sem.at[i, src],
            device_id={"ep": me}, device_id_type=MESH).wait_recv()

    def combine(i):
        for p in range(1, group):
            back_wait(i, owners[p])
        for h in range(H_CHUNKS):
            cols = pl.ds(h * hc, hc)
            parts = dot(w_stack[i], back[i, :, :, cols].reshape(group * MAIN, hc))
            acc[:, cols] = acc[:, cols] + (parts[:tok] + (parts[tok:2 * tok] + parts[2 * tok:]))

    def next_gu_of(i):
        def next_gu(f, slot):
            ahead = (f + GU_SLOTS) // FF_CHUNKS
            f_next = (f + GU_SLOTS) % FF_CHUNKS

            @pl.when(i + ahead < local)
            def _():
                start_gu(i + ahead, f_next, slot, False)

        return next_gu

    def next_d_of(i):
        def next_d(h, slot):
            ahead = D_SLOTS // H_CHUNKS

            @pl.when(i + ahead < local)
            def _():
                d_copy(i + ahead, h, slot, False).start()

        return next_d

    def expert(i, lo, hi, first_pass, last_pass):
        rows = (hi - lo) * MAIN

        def put_out(h, value):
            xo[i, pl.ds(lo, hi - lo), :, pl.ds(h * hc, hc)] = value.astype(BF16).reshape(hi - lo, MAIN, hc)

        unit_step(
            rows, lambda: xo[i, pl.ds(lo, hi - lo)].reshape(rows, hid),
            (i + shared_units) * FF_CHUNKS, (i + shared_units) * H_CHUNKS, put_out,
            next_gu_of(i) if last_pass else None, next_d_of(i) if last_pass else None, not first_pass)
        for p in send_order:
            if lo <= p < hi:
                back_send(i, xo.at[i, p], p).start()
        if lo == 0:
            back[i, me] = xo[i, 0]

    expert(0, 0, near, True, False)
    tail_sum[...] = gather_extra(0) + gather_extra(1) + gather_extra(2)
    x_wait(far, 0)
    start_x(12, 13)
    x_wait(far, 1)
    start_x(13, 14)
    gather_owner(far, near)
    for part in range(2):
        x_wait(owners[7], part)
    gather_owner(owners[7], near + 1)
    xo[:, group] = norm(tail_sum[...] + gather_extra(3)).reshape(local, MAIN, hid)
    expert(0, near, group + 1, False, True)

    def routed_step(i, carry):
        expert(i, 0, group + 1, True, True)

        @pl.when(i >= 2)
        def _():
            combine(i - 2)

        return carry

    lax.fori_loop(1, local, routed_step, 0)

    left_over = xo[:, group].reshape(local * MAIN, hid)
    row, col = iota((local * MAIN, local * MAIN), 0), iota((local * MAIN, local * MAIN), 1)
    source = ((row % MAIN) // extra) * MAIN + (row // MAIN) * extra + row % extra
    reorder = jnp.where(col == source, 1.0, 0.0).astype(BF16)
    tail[...] = dot(reorder, left_over).astype(BF16).reshape(group, MAIN, hid)
    for p in send_order:
        back_send(local, tail.at[p], p).start()
    back[local, me] = tail[0]

    def combine_step(i, carry):
        combine(i)
        return carry

    lax.fori_loop(local - 2, rounds, combine_step, 0)
    normed[...] = acc[...].astype(BF16)
    out_copy = pltpu.make_async_copy(normed, out_hbm, x_sem)
    out_copy.start()

    for slot in range(len(x_sends)):
        x_send(*x_sends[slot], slot).wait_send()
    for r in range(1, group):
        code_send((me + r) % group, r).wait_send()

    def drain(i, carry):
        for p in send_order:
            back_send(i, tail.at[p], p).wait_send()
        return carry

    lax.fori_loop(0, rounds, drain, 0)
    out_copy.wait()


def solution(mesh):
    group = mesh.shape["ep"]

    def local_step(hidden, norm_gain, router_w, topk_idx, w_gate, w_up, w_down, shared_gate, shared_up, shared_down):
        tok, hid = hidden.shape
        top_k = topk_idx.shape[1]
        experts = router_w.shape[1]
        local, _, ff = w_gate.shape
        capacity = 3 * tok * top_k // (2 * experts)
        assert group == 8 and (capacity - MAIN) * local == MAIN and local == group
        rounds = local + 1
        fc, hc = ff // FF_CHUNKS, hid // H_CHUNKS
        any_spec = pl.BlockSpec(memory_space=pl.ANY)
        dma = pltpu.SemaphoreType.DMA
        return pl.pallas_call(
            functools.partial(moe_kernel, group),
            out_shape=jax.ShapeDtypeStruct((tok, hid), BF16),
            in_specs=[any_spec] * 10,
            out_specs=any_spec,
            scratch_shapes=[
                pltpu.VMEM((group, tok, hid), BF16),
                pltpu.VMEM((local, group + 1, MAIN, hid), BF16),
                pltpu.VMEM((rounds, group, MAIN, hid), BF16),
                pltpu.VMEM((group, MAIN, hid), BF16),
                pltpu.VMEM((GU_SLOTS, 2, hid, fc), BF16),
                pltpu.VMEM((D_SLOTS, ff, hc), BF16),
                pltpu.VMEM(((group + 1) * MAIN, ff), BF16),
                pltpu.VMEM((tok, hid), BF16),
                pltpu.VMEM((tok, hid), F32),
                pltpu.VMEM((rounds, 3 * tok, group * MAIN), BF16),
                pltpu.VMEM((group, group, local, tok), F32),
                pltpu.VMEM((group // 2, local * MAIN, 2 * tok), BF16),
                pltpu.VMEM((local * MAIN, hid), F32),
                pltpu.VMEM((hid,), F32),
                pltpu.VMEM((experts, hid), BF16),
                pltpu.VMEM((top_k, tok), jnp.int32),
                dma((3,)),
                dma,
                dma((GU_SLOTS, 2)),
                dma((D_SLOTS,)),
                dma((14,)),
                dma((group, 2)),
                dma((group,)),
                dma((group,)),
                dma((rounds, group - 1)),
                dma((rounds, group)),
            ],
            compiler_params=pltpu.CompilerParams(
                collective_id=0, has_side_effects=True, vmem_limit_bytes=67_000_000),
            name="moe_block",
        )(hidden, norm_gain, router_w.T, topk_idx.T, w_gate, w_up, w_down, shared_gate, shared_up, shared_down)

    token_spec = P(("dp", "ep"), None)
    expert_spec = P("ep", None, None)
    return jax.shard_map(
        local_step,
        mesh=mesh,
        in_specs=(token_spec, P(None), P(None, None), token_spec, expert_spec, expert_spec, expert_spec,
                  P(None, None), P(None, None), P(None, None)),
        out_specs=token_spec,
        check_vma=False,
    )
```

time: 120 us -> 106 us (0.88)
  Pallas kernels: 113 us -> 104 us
  local copies, waits for them, and re-layouts: 6.74 us -> 1.97 us
    pallas_call x1, Pallas kernels: 113 us -> 104 us  [local_step(): pl.pallas_call(functools.partial(moe_kernel, group), out_shape=jax.ShapeD...]
    unnamed x3 -> x1, local copies, waits for them, and re-layouts: 5.43 us -> 1.97 us
    reshape x1 -> x0, local copies, waits for them, and re-layouts: 1.31 us -> none  [local_step(): norm_gain.reshape(1, hid)]
where the time goes in v1:
time: 106 us
  Pallas kernels  104 us (98%)
  local copies, waits for them, and re-layouts  1.97 us (2%)
    pallas_call x1, Pallas kernels, local_step(): pl.pallas_call(functools.partial(moe_kernel, group), out_shape=jax.ShapeD...  104 us

profile of v1, /device:TPU:81, one launch (start us, length us, event | category | flops | bytes accessed | tf_op | source)
XLA Modules:
  0.0 105.5 jit_solution(16649773400977797786)
XLA Ops:
  0.0 103.5 %moe_block.1 = bf16[128,2560]{1,0:T(8,128)(2,1)} custom-call(bf16[128,2560]{1,0:T(8,128)(2,1)} %x_hbm.1, f32[2560]{0:T(1024)} %gain_hbm.1, bf16[64,2560]{1,0:T(8,128)(2,1)} %bitcast.2, s32[6,128]{1,0:T(8,128)} %bitcast.3, bf16[8,2560,1536]{2,1,0:T(8,128)(2,1)} %wg.1, bf16[8,2560,1536]{2,1,0:T(8,128)(2,1)} %wu.1, bf16[8,1536,2560]{2,1,0:T(8,128)(2,1)} %wd.1, ...), custom_call_target="tpu_custom_call" | custom-call | tf_op jit(solution)/shard_map/moe_block/pallas_call | solution.py:395
  103.5 2.0 %copy.12 = bf16[128,2560]{1,0:T(8,128)(2,1)} copy(bf16[128,2560]{1,0:T(8,128)(2,1)} %moe_block.1) | data formatting | bytes 1310720

commit v2 on v1

--- a/solution.py
+++ b/solution.py
@@ -16,6 +16,7 @@
 D_SLOTS = 4
 FF_CHUNKS = 3
 H_CHUNKS = 2
+EARLY = 1
 
 
 def dot(a, b):
@@ -79,10 +80,10 @@
     for r in range(1, group):
         pl.semaphore_signal(barrier, inc=1, device_id={"ep": (me + r) % group}, device_id_type=MESH)
     x_copy.wait()
-    for q in range(GU_SLOTS):
-        start_gu(q // FF_CHUNKS, q % FF_CHUNKS, q, True)
-        if q < D_SLOTS:
-            d_copy(q // H_CHUNKS, q % H_CHUNKS, q, True).start()
+    for q in range(FF_CHUNKS):
+        start_gu(0, q, q, True)
+    for q in range(H_CHUNKS):
+        d_copy(0, q, q, True).start()
 
     for copy in small:
         copy.wait()
@@ -141,6 +142,10 @@
             x_send(*x_sends[slot], slot).start()
 
     start_x(0, 6)
+    for q in range(FF_CHUNKS, GU_SLOTS):
+        start_gu(q // FF_CHUNKS - EARLY, q % FF_CHUNKS, q, False)
+    for q in range(H_CHUNKS, D_SLOTS):
+        d_copy(q // H_CHUNKS - EARLY, q % H_CHUNKS, q, False).start()
 
     logits = lax.dot_general(normed[...], rw_ref[...], (((1,), (1,)), ((), ())), preferred_element_type=F32)
     peak = jnp.max(logits, axis=-1, keepdims=True)
@@ -198,11 +203,6 @@
         return carry
 
     lax.fori_loop(0, 2, gather_home, 0)
-    x_wait(left, 0)
-    start_x(6, 8)
-    x_wait(right, 1)
-    start_x(8, 10)
-
     def unit_step(rows, load_rows, gu_first, d_first, put_out, next_gu=None, next_d=None, arrived=False):
         for f in range(FF_CHUNKS):
             slot = (gu_first + f) % GU_SLOTS
@@ -222,31 +222,48 @@
             if next_d is not None:
                 next_d(h, slot)
 
-    def shared_step(u, carry):
+    def next_gu_of(n):
         def next_gu(f, slot):
-            ahead = (f + GU_SLOTS) // FF_CHUNKS
+            unit = n + (f + GU_SLOTS) // FF_CHUNKS
             f_next = (f + GU_SLOTS) % FF_CHUNKS
 
-            @pl.when(u + ahead < shared_units)
+            @pl.when(unit < local + EARLY)
             def _():
-                start_gu(u + ahead, f_next, slot, True)
-
-            @pl.when(u + ahead >= shared_units)
+                start_gu(unit - EARLY, f_next, slot, False)
+
+            @pl.when((unit >= local + EARLY) & (unit < local + shared_units))
             def _():
-                start_gu(u + ahead - shared_units, f_next, slot, False)
-
+                start_gu(unit - local, f_next, slot, True)
+
+        return next_gu
+
+    def next_d_of(n):
         def next_d(h, slot):
-            d_copy(u + D_SLOTS // H_CHUNKS - shared_units, h, slot, False).start()
-
+            unit = n + D_SLOTS // H_CHUNKS
+
+            @pl.when(unit < local + EARLY)
+            def _():
+                d_copy(unit - EARLY, h, slot, False).start()
+
+            @pl.when((unit >= local + EARLY) & (unit < local + shared_units))
+            def _():
+                d_copy(unit - local, h, slot, True).start()
+
+        return next_d
+
+    def shared_unit(n):
         def put_out(h, value):
             cols = pl.ds(h * hc, hc)
             acc[:, cols] = acc[:, cols] + value
 
-        unit_step(tok, lambda: normed[...], u * FF_CHUNKS, u * H_CHUNKS, put_out, next_gu, next_d)
-
-        return carry
-
-    lax.fori_loop(0, shared_units, shared_step, 0)
+        unit_step(tok, lambda: normed[...], n * FF_CHUNKS, n * H_CHUNKS, put_out, next_gu_of(n), next_d_of(n))
+
+    for n in range(EARLY):
+        shared_unit(n)
+    x_wait(left, 0)
+    start_x(6, 8)
+    x_wait(right, 1)
+    start_x(8, 10)
     x_wait(left, 1)
     start_x(10, 11)
     x_wait(right, 0)
@@ -285,37 +302,17 @@
             parts = dot(w_stack[i], back[i, :, :, cols].reshape(group * MAIN, hc))
             acc[:, cols] = acc[:, cols] + (parts[:tok] + (parts[tok:2 * tok] + parts[2 * tok:]))
 
-    def next_gu_of(i):
-        def next_gu(f, slot):
-            ahead = (f + GU_SLOTS) // FF_CHUNKS
-            f_next = (f + GU_SLOTS) % FF_CHUNKS
-
-            @pl.when(i + ahead < local)
-            def _():
-                start_gu(i + ahead, f_next, slot, False)
-
-        return next_gu
-
-    def next_d_of(i):
-        def next_d(h, slot):
-            ahead = D_SLOTS // H_CHUNKS
-
-            @pl.when(i + ahead < local)
-            def _():
-                d_copy(i + ahead, h, slot, False).start()
-
-        return next_d
-
     def expert(i, lo, hi, first_pass, last_pass):
         rows = (hi - lo) * MAIN
+        n = i + EARLY
 
         def put_out(h, value):
             xo[i, pl.ds(lo, hi - lo), :, pl.ds(h * hc, hc)] = value.astype(BF16).reshape(hi - lo, MAIN, hc)
 
         unit_step(
             rows, lambda: xo[i, pl.ds(lo, hi - lo)].reshape(rows, hid),
-            (i + shared_units) * FF_CHUNKS, (i + shared_units) * H_CHUNKS, put_out,
-            next_gu_of(i) if last_pass else None, next_d_of(i) if last_pass else None, not first_pass)
+            n * FF_CHUNKS, n * H_CHUNKS, put_out,
+            next_gu_of(n) if last_pass else None, next_d_of(n) if last_pass else None, not first_pass)
         for p in send_order:
             if lo <= p < hi:
                 back_send(i, xo.at[i, p], p).start()
@@ -335,12 +332,14 @@
     xo[:, group] = norm(tail_sum[...] + gather_extra(3)).reshape(local, MAIN, hid)
     expert(0, near, group + 1, False, True)
 
+    lag = 3
+
     def routed_step(i, carry):
         expert(i, 0, group + 1, True, True)
 
-        @pl.when(i >= 2)
+        @pl.when(i >= lag)
         def _():
-            combine(i - 2)
+            combine(i - lag)
 
         return carry
 
@@ -355,11 +354,14 @@
         back_send(local, tail.at[p], p).start()
     back[local, me] = tail[0]
 
+    for n in range(local + EARLY, local + shared_units):
+        shared_unit(n)
+
     def combine_step(i, carry):
         combine(i)
         return carry
 
-    lax.fori_loop(local - 2, rounds, combine_step, 0)
+    lax.fori_loop(local - lag, rounds, combine_step, 0)
     normed[...] = acc[...].astype(BF16)
     out_copy = pltpu.make_async_copy(normed, out_hbm, x_sem)
     out_copy.start()

time: 106 us -> 104 us (0.981)
  Pallas kernels: 104 us -> 102 us
    pallas_call x1, Pallas kernels: 104 us -> 102 us  [local_step(): pl.pallas_call(functools.partial(moe_kernel, group), out_shape=jax.ShapeD...]
where the time goes in v2:
time: 104 us
  Pallas kernels  102 us (98%)
  local copies, waits for them, and re-layouts  1.97 us (2%)
    pallas_call x1, Pallas kernels, local_step(): pl.pallas_call(functools.partial(moe_kernel, group), out_shape=jax.ShapeD...  102 us

profile of v2, /device:TPU:81, one launch (start us, length us, event | category | flops | bytes accessed | tf_op | source)
XLA Modules:
  0.0 104.2 jit_solution(9262197479813189544)
XLA Ops:
  0.0 102.3 %moe_block.1 = bf16[128,2560]{1,0:T(8,128)(2,1)} custom-call(bf16[128,2560]{1,0:T(8,128)(2,1)} %x_hbm.1, f32[2560]{0:T(1024)} %gain_hbm.1, bf16[64,2560]{1,0:T(8,128)(2,1)} %bitcast.2, s32[6,128]{1,0:T(8,128)} %bitcast.3, bf16[8,2560,1536]{2,1,0:T(8,128)(2,1)} %wg.1, bf16[8,2560,1536]{2,1,0:T(8,128)(2,1)} %wu.1, bf16[8,1536,2560]{2,1,0:T(8,128)(2,1)} %wd.1, ...), custom_call_target="tpu_custom_call" | custom-call | tf_op jit(solution)/shard_map/moe_block/pallas_call | solution.py:397
  102.3 2.0 %copy.12 = bf16[128,2560]{1,0:T(8,128)(2,1)} copy(bf16[128,2560]{1,0:T(8,128)(2,1)} %moe_block.1) | data formatting | bytes 1310720
